TPU v7x, 128 devices: a whole 4x4x4 slice. The times are simulated.
128 devices in a mesh: dap: 128 (over x, y, z, core).
Axes of the slice: x: 4, y: 4, z: 4, core: 2. Of those that a mesh axis runs over, the one named last changes fastest.
Arguments:
- pair: bfloat16 [512, 512, 128], P('dap'), may hold values from -6 to 6
- residue_mask: int32 [512], P('dap'), may hold values 0 or 1
- norm_gain: float32 [2, 128], replicated, may hold values from 0.5 to 1.5
- proj_weight: bfloat16 [2, 128, 512], replicated, may hold values from -0.5 to 0.5
- gate_weight: bfloat16 [2, 128, 128], replicated, may hold values from -0.5 to 0.5
- mix_gain: float32 [2, 128], replicated, may hold values from 0.5 to 1.5
- out_weight: bfloat16 [2, 128, 128], replicated, may hold values from -0.5 to 0.5
Outputs:
- updated_pair: bfloat16 [512, 512, 128], P('dap')
All inputs are finite; a program needn't handle non-finite values. No bound on the sum of `residue_mask` on one device may be relied on, other than what follows from the above.
Results may differ from a plain program's by a relative error of at most 0.0061.
Values may be sent and summed in bfloat16 or wider, within the bound.
A program may use at most 64 MiB of HBM per device.

v0:
```python
import functools

import jax
import jax.numpy as jnp
from jax import lax
from jax.experimental import pallas as pl
from jax.experimental.pallas import tpu as pltpu
from jax.sharding import PartitionSpec as P

EPS = 1e-05
ND = 128
MESH = pl.DeviceIdType.MESH
F32 = jnp.float32
BF16 = jnp.bfloat16


def offset_order():
    offs = [(a, b, c, d) for a in range(4) for b in range(4) for c in range(4) for d in range(2)][1:]
    offs.sort(key=lambda o: -sum(min(v, 4 - v) for v in o[:3]))
    groups = {}
    for o in offs:
        key = next(((a, o[a]) for a in range(3) if o[a]), (3, 0))
        groups.setdefault(key, []).append(o)
    timed = [((i + 0.5) / len(g), o) for g in groups.values() for i, o in enumerate(g)]
    timed.sort(key=lambda t: t[0])
    return [o for _, o in timed]


ORDER = offset_order()


def sigmoid(v):
    return 0.5 * jnp.tanh(0.5 * v) + 0.5


def normalize(v):
    center = v - jnp.mean(v, axis=0, keepdims=True)
    spread = jnp.mean(center * center, axis=0, keepdims=True)
    return center * lax.rsqrt(spread + EPS)


def kernel(
    pair, mask, norm_gain, proj_w, gate_w, mix_gain, out_w, out,
    xt, nt, wt, gwt, owt, gains, flat, send, recv, tsend, trecv, mat_a, mat_b, msend, mrecv, mrow,
    ssem, rsem,
):
    me = lax.axis_index("dap")
    core, z = lax.rem(me, 2), lax.rem(me // 2, 4)
    y, x = lax.rem(me // 8, 4), me // 32
    xs = [lax.rem(x + d, 4) * 32 for d in range(4)]
    ys = [lax.rem(y + d, 4) * 8 for d in range(4)]
    zs = [lax.rem(z + d, 4) * 2 for d in range(4)]
    cs = [lax.rem(core + d, 2) for d in range(2)]
    peers = [xs[a] + ys[b] + zs[c] + cs[d] for a, b, c, d in ORDER]

    barrier = pltpu.get_barrier_semaphore()
    for peer in peers:
        pl.semaphore_signal(barrier, inc=1, device_id=(peer,), device_id_type=MESH)

    for u in range(2):
        wt[u] = proj_w[u].astype(F32).T.astype(BF16)
        gwt[u] = gate_w[u].astype(F32).T.astype(BF16)
        owt[u] = out_w[u].astype(F32).T.astype(BF16)
        gains[0, u] = jnp.broadcast_to(norm_gain[u : u + 1, :], (128, 128)).T
        gains[1, u] = jnp.broadcast_to(mix_gain[u : u + 1, :], (128, 128)).T

    lane = lax.broadcasted_iota(jnp.int32, (1, 128), 1)
    base = lax.rem(me, 32) * 4
    row = jnp.zeros((1, 128), F32)
    for r in range(4):
        row = jnp.where(lane == base + r, mask[0, r].astype(F32), row)
    msend[...] = row

    def load_pair(s, _):
        at = pl.multiple_of(s * 128, 128)
        xt[:, pl.ds(at, 128)] = pair[s // 4, pl.ds(pl.multiple_of(lax.rem(s, 4) * 128, 128), 128), :].astype(F32).T
        return 0

    lax.fori_loop(0, 16, load_pair, 0)

    def panel_step(u, s):
        at = pl.multiple_of(s * 128, 128)
        normed = (normalize(xt[:, pl.ds(at, 128)]) * gains[0, u]).astype(BF16)
        nt[:, pl.ds(at, 128)] = normed
        keep = mask[0, s // 4].astype(F32)
        if u == 1:
            keep = keep * mrow[pl.ds(lax.rem(s, 4), 1), :]
        for p in range(2):
            proj = jnp.dot(wt[u, p * 256 : p * 256 + 256, :], normed, preferred_element_type=F32)
            flat[p, pl.ds(s, 128, stride=16), :] = sigmoid(proj[:128]) * proj[128:] * keep

    def pack(u):
        def step(c, _):
            for p in range(2):
                rows = flat[p, pl.ds(pl.multiple_of(c * 128, 128), 128), :]
                send[u, pl.ds(c * 8, 8), p] = rows.astype(BF16).reshape(8, 16, 128)
            return 0

        lax.fori_loop(0, 16, step, 0)

    def exchange(k, src, dst):
        for peer in peers:
            pltpu.make_async_remote_copy(
                src.at[peer], dst.at[me], ssem.at[k], rsem.at[k], device_id=(peer,), device_id_type=MESH
            ).start()
        dst[me] = src[me]

    def arrived(k, dst):
        part = dst.at[pl.ds(0, ND - 1)]
        pltpu.make_async_copy(part, part, rsem.at[k]).wait()

    def sent(k, src):
        part = src.at[pl.ds(0, ND - 1)]
        pltpu.make_async_copy(part, part, ssem.at[k]).wait()

    def products(u):
        def spread(d, _):
            for p in range(2):
                rows = recv[u, pl.ds(d * 8, 8), p].reshape(128, 128).astype(F32)
                flat[p, pl.ds(pl.multiple_of(d * 128, 128), 128), :] = rows
            return 0

        lax.fori_loop(0, 16, spread, 0)
        for q in range(4):
            left = flat[0, pl.ds(q, 512, stride=4), :]
            right = flat[1, pl.ds(q, 512, stride=4), :]
            if u == 0:
                mat_a[:, q * 128 : q * 128 + 128] = (left * mrow[q : q + 1, :]).astype(BF16)
            else:
                mat_a[q * 128 : q * 128 + 128, :] = left.T.astype(BF16)
            mat_b[:, q * 128 : q * 128 + 128] = right.astype(BF16)
        for q in range(4):
            if u == 0:
                tri = lax.dot_general(
                    mat_a[...], mat_b[q * 128 : q * 128 + 128, :], (((1,), (1,)), ((), ())), preferred_element_type=F32
                )
            else:
                tri = jnp.dot(mat_a[...], mat_b[:, q * 128 : q * 128 + 128], preferred_element_type=F32)
            flat[0, pl.ds(q, 512, stride=4), :] = tri

        def gather(d, _):
            rows = flat[0, pl.ds(pl.multiple_of(d * 128, 128), 128), :]
            tsend[u, pl.ds(d * 8, 8)] = rows.astype(BF16).reshape(8, 16, 128)
            return 0

        lax.fori_loop(0, 16, gather, 0)

    def unpack(u):
        def step(c, _):
            rows = trecv[u, pl.ds(c * 8, 8)].reshape(128, 128).astype(F32)
            flat[0, pl.ds(pl.multiple_of(c * 128, 128), 128), :] = rows
            return 0

        lax.fori_loop(0, 16, step, 0)

    def finish_step(u, s):
        at = pl.multiple_of(s * 128, 128)
        tri = flat[0, pl.ds(s, 128, stride=16), :]
        normed = (normalize(tri) * gains[1, u]).astype(BF16)
        result = jnp.dot(owt[u], normed, preferred_element_type=F32)
        gate = sigmoid(jnp.dot(gwt[u], nt[:, pl.ds(at, 128)], preferred_element_type=F32))
        return at, (xt[:, pl.ds(at, 128)] + gate * result).astype(BF16).astype(F32)

    def first_panels(s, _):
        panel_step(0, s)
        return 0

    lax.fori_loop(0, 16, first_panels, 0)
    pack(0)
    pl.semaphore_wait(barrier, ND - 1)
    for peer in peers:
        pltpu.make_async_remote_copy(
            msend, mrecv.at[me], ssem.at[4], rsem.at[4], device_id=(peer,), device_id_type=MESH
        ).start()
    mrecv[me] = msend[...]
    exchange(0, send.at[0], recv.at[0])
    arrived(4, mrecv)
    for q in range(4):
        mrow[q : q + 1, :] = jnp.sum(mrecv[q * 32 : q * 32 + 32], axis=0)
    arrived(0, recv.at[0])
    products(0)
    exchange(1, tsend.at[0], trecv.at[0])
    arrived(1, trecv.at[0])
    unpack(0)

    def middle(s, _):
        at, value = finish_step(0, s)
        xt[:, pl.ds(at, 128)] = value
        return 0

    lax.fori_loop(0, 16, middle, 0)

    def second_panels(s, _):
        panel_step(1, s)
        return 0

    lax.fori_loop(0, 16, second_panels, 0)
    pack(1)
    exchange(2, send.at[1], recv.at[1])
    arrived(2, recv.at[1])
    products(1)
    exchange(3, tsend.at[1], trecv.at[1])
    arrived(3, trecv.at[1])
    unpack(1)

    def last(s, _):
        _, value = finish_step(1, s)
        out[s // 4, pl.ds(pl.multiple_of(lax.rem(s, 4) * 128, 128), 128), :] = value.T.astype(BF16)
        return 0

    lax.fori_loop(0, 16, last, 0)
    sent(4, mrecv)
    sent(0, send.at[0])
    sent(1, tsend.at[0])
    sent(2, send.at[1])
    sent(3, tsend.at[1])


def body(pair, residue_mask, norm_gain, proj_weight, gate_weight, mix_gain, out_weight):
    vmem = pl.BlockSpec(memory_space=pltpu.VMEM)
    return pl.pallas_call(
        kernel,
        out_shape=jax.ShapeDtypeStruct((4, 512, 128), BF16),
        in_specs=[vmem, pl.BlockSpec(memory_space=pltpu.SMEM)] + [vmem] * 5,
        out_specs=vmem,
        scratch_shapes=[
            pltpu.VMEM((128, 2048), F32),
            pltpu.VMEM((128, 2048), BF16),
            pltpu.VMEM((2, 512, 128), BF16),
            pltpu.VMEM((2, 128, 128), BF16),
            pltpu.VMEM((2, 128, 128), BF16),
            pltpu.VMEM((2, 2, 128, 128), F32),
            pltpu.VMEM((2, 2048, 128), F32),
            pltpu.VMEM((2, ND, 2, 16, 128), BF16),
            pltpu.VMEM((2, ND, 2, 16, 128), BF16),
            pltpu.VMEM((2, ND, 16, 128), BF16),
            pltpu.VMEM((2, ND, 16, 128), BF16),
            pltpu.VMEM((512, 512), BF16),
            pltpu.VMEM((512, 512), BF16),
            pltpu.VMEM((1, 128), F32),
            pltpu.VMEM((ND, 1, 128), F32),
            pltpu.VMEM((4, 128), F32),
            pltpu.SemaphoreType.DMA((5,)),
            pltpu.SemaphoreType.DMA((5,)),
        ],
        compiler_params=pltpu.CompilerParams(collective_id=0, has_side_effects=True, vmem_limit_bytes=48 << 20),
    )(pair, residue_mask.reshape(1, 4), norm_gain, proj_weight, gate_weight, mix_gain, out_weight)


def solution(mesh):
    in_specs = (P("dap", None, None), P("dap"), P(), P(), P(), P(), P())
    return jax.shard_map(body, mesh=mesh, in_specs=in_specs, out_specs=P("dap", None, None), check_vma=False)
```

profile of v0, /device:TPU:1, one launch (start us, length us, event | category | flops | bytes accessed | tf_op | source)
XLA Modules:
  0.0 83.6 jit_solution(1432001439213750181)
XLA Ops:
  0.0 0.0 copy-start.4
  0.0 0.0 copy-start.6
  0.0 0.7 copy-done.4
  0.7 0.0 copy-done.6
  0.7 0.0 copy-start
  0.7 1.0 %copy-done = bf16[4,512,128]{2,1,0:T(8,128)(2,1)S(1)} copy-done((bf16[4,512,128]{2,1,0:T(8,128)(2,1)S(1)}, bf16[4,512,128]{2,1,0:T(8,128)(2,1)}, u32[]{:S(2)}) %copy-start) | copy-done | bytes 524312
  1.7 0.0 copy-start.1
  1.7 0.9 %copy-done.1 = bf16[2,128,512]{2,1,0:T(8,128)(2,1)S(1)} copy-done((bf16[2,128,512]{2,1,0:T(8,128)(2,1)S(1)}, bf16[2,128,512]{2,1,0:T(8,128)(2,1)}, u32[]{:S(2)}) %copy-start.1) | copy-done | bytes 262168
  2.7 0.0 copy-start.2
  2.7 0.8 %copy-done.2 = bf16[2,128,128]{2,1,0:T(8,128)(2,1)S(1)} copy-done((bf16[2,128,128]{2,1,0:T(8,128)(2,1)S(1)}, bf16[2,128,128]{2,1,0:T(8,128)(2,1)}, u32[]{:S(2)}) %copy-start.2) | copy-done | bytes 65560
  3.5 0.0 copy-start.3
  3.5 0.8 %copy-done.3 = bf16[2,128,128]{2,1,0:T(8,128)(2,1)S(1)} copy-done((bf16[2,128,128]{2,1,0:T(8,128)(2,1)S(1)}, bf16[2,128,128]{2,1,0:T(8,128)(2,1)}, u32[]{:S(2)}) %copy-start.3) | copy-done | bytes 65560
  4.4 0.0 copy-start.5
  4.4 0.7 copy-done.5
  5.0 77.8 %shard_map.73 = bf16[4,512,128]{2,1,0:T(8,128)(2,1)S(1)} custom-call(bf16[4,512,128]{2,1,0:T(8,128)(2,1)S(1)} %copy-done, s32[1,4]{1,0:T(1,128)S(1)} %bitcast.1, f32[2,128]{1,0:T(2,128)S(1)} %copy-done.4, bf16[2,128,512]{2,1,0:T(8,128)(2,1)S(1)} %copy-done.1, bf16[2,128,128]{2,1,0:T(8,128)(2,1)S(1)} %copy-done.2, f32[2,128]{1,0:T(2,128)S(1)} %copy-done.5, ...), custom_call_target="tpu_custom_call" | custom-call | tf_op jit(solution)/shard_map/pallas_call | solution.py:221
  82.8 0.8 copy.9
Async XLA Ops:
  0.0 0.7 copy-start.4
  0.0 0.7 copy-start.6
  0.7 1.0 %copy-start = (bf16[4,512,128]{2,1,0:T(8,128)(2,1)S(1)}, bf16[4,512,128]{2,1,0:T(8,128)(2,1)}, u32[]{:S(2)}) copy-start(bf16[4,512,128]{2,1,0:T(8,128)(2,1)} %pair.1) | copy-start | bytes 1572868
  1.7 0.9 %copy-start.1 = (bf16[2,128,512]{2,1,0:T(8,128)(2,1)S(1)}, bf16[2,128,512]{2,1,0:T(8,128)(2,1)}, u32[]{:S(2)}) copy-start(bf16[2,128,512]{2,1,0:T(8,128)(2,1)} %proj_w.1) | copy-start | bytes 786436
  2.7 0.8 %copy-start.2 = (bf16[2,128,128]{2,1,0:T(8,128)(2,1)S(1)}, bf16[2,128,128]{2,1,0:T(8,128)(2,1)}, u32[]{:S(2)}) copy-start(bf16[2,128,128]{2,1,0:T(8,128)(2,1)} %gate_w.1) | copy-start | bytes 196612
  3.5 0.8 %copy-start.3 = (bf16[2,128,128]{2,1,0:T(8,128)(2,1)S(1)}, bf16[2,128,128]{2,1,0:T(8,128)(2,1)}, u32[]{:S(2)}) copy-start(bf16[2,128,128]{2,1,0:T(8,128)(2,1)} %out_w.1) | copy-start | bytes 196612
  4.4 0.7 copy-start.5
where the time goes:
time: 83.9 us; the launch traced here: 83.6 us
  Pallas kernels  77.8 us (93%)
  local copies, waits for them, and re-layouts  5.82 us (7%)
    pallas_call x1, Pallas kernels, body(): pl.pallas_call(kernel, out_shape=jax.ShapeDtypeStruct((4, 512, 128), BF16...  77.8 us
    unnamed x15, local copies, waits for them, and re-layouts  5.82 us

commit v1 on v0

--- a/solution.py
+++ b/solution.py
@@ -40,10 +40,17 @@
 
 
 def kernel(
-    pair, mask, norm_gain, proj_w, gate_w, mix_gain, out_w, out,
-    xt, nt, wt, gwt, owt, gains, flat, send, recv, tsend, trecv, mat_a, mat_b, msend, mrecv, mrow,
+    pair_h, mask, norm_gain_h, proj_w_h, gate_w_h, mix_gain_h, out_w_h, out,
+    pair, norm_gain, proj_w, gate_w, mix_gain, out_w, isem, xt, nt, wt, gwt, owt, gains, flat, send, recv, tsend, trecv, mat_a, mat_b, msend, mrecv, mrow,
     ssem, rsem,
 ):
+    pairs = (
+        (pair_h, pair), (norm_gain_h, norm_gain), (proj_w_h, proj_w),
+        (gate_w_h, gate_w), (mix_gain_h, mix_gain), (out_w_h, out_w),
+    )
+    loads = [pltpu.make_async_copy(a, b, isem.at[i]) for i, (a, b) in enumerate(pairs)]
+    for load in loads:
+        load.start()
     me = lax.axis_index("dap")
     core, z = lax.rem(me, 2), lax.rem(me // 2, 4)
     y, x = lax.rem(me // 8, 4), me // 32
@@ -57,6 +64,8 @@
     for peer in peers:
         pl.semaphore_signal(barrier, inc=1, device_id=(peer,), device_id_type=MESH)
 
+    for load in loads:
+        load.wait()
     for u in range(2):
         wt[u] = proj_w[u].astype(F32).T.astype(BF16)
         gwt[u] = gate_w[u].astype(F32).T.astype(BF16)
@@ -71,23 +80,25 @@
         row = jnp.where(lane == base + r, mask[0, r].astype(F32), row)
     msend[...] = row
 
-    def load_pair(s, _):
-        at = pl.multiple_of(s * 128, 128)
-        xt[:, pl.ds(at, 128)] = pair[s // 4, pl.ds(pl.multiple_of(lax.rem(s, 4) * 128, 128), 128), :].astype(F32).T
-        return 0
-
-    lax.fori_loop(0, 16, load_pair, 0)
-
-    def panel_step(u, s):
-        at = pl.multiple_of(s * 128, 128)
-        normed = (normalize(xt[:, pl.ds(at, 128)]) * gains[0, u]).astype(BF16)
-        nt[:, pl.ds(at, 128)] = normed
-        keep = mask[0, s // 4].astype(F32)
-        if u == 1:
-            keep = keep * mrow[pl.ds(lax.rem(s, 4), 1), :]
-        for p in range(2):
-            proj = jnp.dot(wt[u, p * 256 : p * 256 + 256, :], normed, preferred_element_type=F32)
-            flat[p, pl.ds(s, 128, stride=16), :] = sigmoid(proj[:128]) * proj[128:] * keep
+    for r in range(4):
+        xt[:, r * 512 : r * 512 + 512] = pair[r].astype(F32).T
+
+    def tiled(column, times):
+        return jnp.concatenate([column] * times, axis=1)
+
+    def panels(u):
+        for r in range(4):
+            at = slice(r * 512, r * 512 + 512)
+            normed = (normalize(xt[:, at]) * tiled(gains[0, u], 4)).astype(BF16)
+            nt[:, at] = normed
+            keep = mask[0, r].astype(F32)
+            if u == 1:
+                keep = keep * jnp.concatenate([mrow[q : q + 1, :] for q in range(4)], axis=1)
+            for p in range(2):
+                proj = jnp.dot(wt[u, p * 256 : p * 256 + 256, :], normed, preferred_element_type=F32)
+                value = sigmoid(proj[:128]) * proj[128:] * keep
+                for q in range(4):
+                    flat[p, pl.ds(r * 4 + q, 128, stride=16), :] = value[:, q * 128 : q * 128 + 128]
 
     def pack(u):
         def step(c, _):
@@ -153,19 +164,16 @@
 
         lax.fori_loop(0, 16, step, 0)
 
-    def finish_step(u, s):
-        at = pl.multiple_of(s * 128, 128)
-        tri = flat[0, pl.ds(s, 128, stride=16), :]
-        normed = (normalize(tri) * gains[1, u]).astype(BF16)
-        result = jnp.dot(owt[u], normed, preferred_element_type=F32)
-        gate = sigmoid(jnp.dot(gwt[u], nt[:, pl.ds(at, 128)], preferred_element_type=F32))
-        return at, (xt[:, pl.ds(at, 128)] + gate * result).astype(BF16).astype(F32)
-
-    def first_panels(s, _):
-        panel_step(0, s)
-        return 0
-
-    lax.fori_loop(0, 16, first_panels, 0)
+    def finish(u, put):
+        for r in range(4):
+            at = slice(r * 512, r * 512 + 512)
+            tri = jnp.concatenate([flat[0, pl.ds(r * 4 + q, 128, stride=16), :] for q in range(4)], axis=1)
+            normed = (normalize(tri) * tiled(gains[1, u], 4)).astype(BF16)
+            result = jnp.dot(owt[u], normed, preferred_element_type=F32)
+            gate = sigmoid(jnp.dot(gwt[u], nt[:, at], preferred_element_type=F32))
+            put(r, at, xt[:, at] + gate * result)
+
+    panels(0)
     pack(0)
     pl.semaphore_wait(barrier, ND - 1)
     for peer in peers:
@@ -183,18 +191,11 @@
     arrived(1, trecv.at[0])
     unpack(0)
 
-    def middle(s, _):
-        at, value = finish_step(0, s)
-        xt[:, pl.ds(at, 128)] = value
-        return 0
-
-    lax.fori_loop(0, 16, middle, 0)
-
-    def second_panels(s, _):
-        panel_step(1, s)
-        return 0
-
-    lax.fori_loop(0, 16, second_panels, 0)
+    def middle(r, at, value):
+        xt[:, at] = value.astype(BF16).astype(F32)
+
+    finish(0, middle)
+    panels(1)
     pack(1)
     exchange(2, send.at[1], recv.at[1])
     arrived(2, recv.at[1])
@@ -203,12 +204,10 @@
     arrived(3, trecv.at[1])
     unpack(1)
 
-    def last(s, _):
-        _, value = finish_step(1, s)
-        out[s // 4, pl.ds(pl.multiple_of(lax.rem(s, 4) * 128, 128), 128), :] = value.T.astype(BF16)
-        return 0
-
-    lax.fori_loop(0, 16, last, 0)
+    def last(r, at, value):
+        out[r] = value.T.astype(BF16)
+
+    finish(1, last)
     sent(4, mrecv)
     sent(0, send.at[0])
     sent(1, tsend.at[0])
@@ -217,13 +216,20 @@
 
 
 def body(pair, residue_mask, norm_gain, proj_weight, gate_weight, mix_gain, out_weight):
-    vmem = pl.BlockSpec(memory_space=pltpu.VMEM)
+    vmem, hbm = pl.BlockSpec(memory_space=pltpu.VMEM), pl.BlockSpec(memory_space=pltpu.HBM)
     return pl.pallas_call(
         kernel,
         out_shape=jax.ShapeDtypeStruct((4, 512, 128), BF16),
-        in_specs=[vmem, pl.BlockSpec(memory_space=pltpu.SMEM)] + [vmem] * 5,
+        in_specs=[hbm, pl.BlockSpec(memory_space=pltpu.SMEM)] + [hbm] * 5,
         out_specs=vmem,
         scratch_shapes=[
+            pltpu.VMEM((4, 512, 128), BF16),
+            pltpu.VMEM((2, 128), F32),
+            pltpu.VMEM((2, 128, 512), BF16),
+            pltpu.VMEM((2, 128, 128), BF16),
+            pltpu.VMEM((2, 128), F32),
+            pltpu.VMEM((2, 128, 128), BF16),
+            pltpu.SemaphoreType.DMA((6,)),
             pltpu.VMEM((128, 2048), F32),
             pltpu.VMEM((128, 2048), BF16),
             pltpu.VMEM((2, 512, 128), BF16),
@@ -243,7 +249,7 @@
             pltpu.SemaphoreType.DMA((5,)),
             pltpu.SemaphoreType.DMA((5,)),
         ],
-        compiler_params=pltpu.CompilerParams(collective_id=0, has_side_effects=True, vmem_limit_bytes=48 << 20),
+        compiler_params=pltpu.CompilerParams(collective_id=0, has_side_effects=True, vmem_limit_bytes=67_043_328),
     )(pair, residue_mask.reshape(1, 4), norm_gain, proj_weight, gate_weight, mix_gain, out_weight)
 
 

time: 83.9 us -> 67.8 us (0.81)
  Pallas kernels: 77.8 us -> 65.8 us
  local copies, waits for them, and re-layouts: 5.82 us -> 1.87 us
    pallas_call x1, Pallas kernels: 77.8 us -> 65.8 us  [body(): pl.pallas_call(kernel, out_shape=jax.ShapeDtypeStruct((4, 512, 128), BF16...]
    unnamed x15 -> x1, local copies, waits for them, and re-layouts: 5.82 us -> 1.87 us
where the time goes in v1:
time: 67.8 us; the launch traced here: 67.7 us
  Pallas kernels  65.8 us (97%)
  local copies, waits for them, and re-layouts  1.87 us (3%)
    pallas_call x1, Pallas kernels, body(): pl.pallas_call(kernel, out_shape=jax.ShapeDtypeStruct((4, 512, 128), BF16...  65.8 us
    unnamed x1, local copies, waits for them, and re-layouts  1.87 us

profile of v1, /device:TPU:1, one launch (start us, length us, event | category | flops | bytes accessed | tf_op | source)
XLA Modules:
  0.0 67.7 jit_solution(7167790187016188355)
XLA Ops:
  0.0 65.8 %shard_map.73 = bf16[4,512,128]{2,1,0:T(8,128)(2,1)} custom-call(bf16[4,512,128]{2,1,0:T(8,128)(2,1)} %pair_h.1, s32[1,4]{1,0:T(1,128)} %bitcast.1, f32[2,128]{1,0:T(2,128)} %norm_gain_h.1, bf16[2,128,512]{2,1,0:T(8,128)(2,1)} %proj_w_h.1, bf16[2,128,128]{2,1,0:T(8,128)(2,1)} %gate_w_h.1, f32[2,128]{1,0:T(2,128)} %mix_gain_h.1, bf16[2,128,128]{2,1,0:T(8,128)(2,1)} %out_w_h.1), custom_call_target="tpu_custom_call" | custom-call | tf_op jit(solution)/shard_map/pallas_call | solution.py:220
  65.8 1.9 %copy.9 = bf16[4,512,128]{2,1,0:T(8,128)(2,1)} copy(bf16[4,512,128]{2,1,0:T(8,128)(2,1)} %shard_map.73) | data formatting | bytes 1048576

commit v2 on v1

v2 whole, which is shorter than its diff:
```python
import jax
import jax.numpy as jnp
from jax import lax
from jax.experimental import pallas as pl
from jax.experimental.pallas import tpu as pltpu
from jax.sharding import PartitionSpec as P

EPS = 1e-05
ND = 128
MESH = pl.DeviceIdType.MESH
F32 = jnp.float32
BF16 = jnp.bfloat16
R0, L0, T0, R1, L1, T1, MASK, KINDS = 0, 1, 5, 9, 13, 17, 21, 22


def sigmoid(v):
    return 0.5 * jnp.tanh(0.5 * v) + 0.5


def normalize(v):
    center = v - jnp.mean(v, axis=0, keepdims=True)
    spread = jnp.mean(center * center, axis=0, keepdims=True)
    return center * lax.rsqrt(spread + EPS)


def tiled(column):
    return jnp.concatenate([column] * 4, axis=1)


def offset_order():
    offs = [(a, b, c, d) for a in range(4) for b in range(4) for c in range(4) for d in range(2)][1:]
    offs.sort(key=lambda o: -sum(min(v, 4 - v) for v in o[:3]))
    groups = {}
    for o in offs:
        key = next(((a, o[a]) for a in range(3) if o[a]), (3, 0))
        groups.setdefault(key, []).append(o)
    timed = [((i + 0.5) / len(g), o) for g in groups.values() for i, o in enumerate(g)]
    timed.sort(key=lambda t: t[0])
    return [o for _, o in timed]


ORDER = offset_order()


def kernel(
    pair_h, mask, norm_gain_h, proj_w_h, gate_w_h, mix_gain_h, out_w_h, out_h,
    pair, norm_gain, proj_w, gate_w, mix_gain, out_w, isem,
    xt, nt, wt, gwt, owt, gains, flat, mat_a, mat_b, msend, mrecv, mrow,
    r0_send, r0_recv, l0_send, l0_recv, t0_send, t0_recv, r1_send, r1_recv, l1_send, l1_recv, t1_send, t1_recv,
    ssem, rsem,
):
    pairs = (
        (pair_h, pair), (proj_w_h, proj_w), (norm_gain_h, norm_gain),
        (gate_w_h, gate_w), (mix_gain_h, mix_gain), (out_w_h, out_w),
    )
    loads = [pltpu.make_async_copy(a, b, isem.at[i]) for i, (a, b) in enumerate(pairs)]
    for load in loads:
        load.start()
    me = lax.axis_index("dap")
    core, z = lax.rem(me, 2), lax.rem(me // 2, 4)
    y, x = lax.rem(me // 8, 4), me // 32
    xs = [lax.rem(x + d, 4) * 32 for d in range(4)]
    ys = [lax.rem(y + d, 4) * 8 for d in range(4)]
    zs = [lax.rem(z + d, 4) * 2 for d in range(4)]
    cs = [lax.rem(core + d, 2) for d in range(2)]
    peers = [xs[a] + ys[b] + zs[c] + cs[d] for a, b, c, d in ORDER]

    def to_all(send_one):
        for peer in peers:
            send_one(peer)

    barrier = pltpu.get_barrier_semaphore()
    to_all(lambda peer: pl.semaphore_signal(barrier, inc=1, device_id=(peer,), device_id_type=MESH))

    def exchange(k, src, dst):
        to_all(
            lambda peer: pltpu.make_async_remote_copy(
                src.at[peer], dst.at[me], ssem.at[k], rsem.at[k], device_id=(peer,), device_id_type=MESH
            ).start()
        )
        dst[me] = src[me]

    def arrived(k, dst):
        part = dst.at[pl.ds(0, ND - 1)]
        pltpu.make_async_copy(part, part, rsem.at[k]).wait()

    def sent(k, src):
        part = src.at[pl.ds(0, ND - 1)]
        pltpu.make_async_copy(part, part, ssem.at[k]).wait()

    def pack(base, rows, dst):
        per = 128 // rows
        for c in range(rows):
            dst[pl.ds(c * per, per)] = flat[pl.ds(base + c * 128, 128), :].astype(BF16).reshape(per, rows, 128)

    def unpack(base, rows, src):
        per = 128 // rows
        for c in range(rows):
            flat[pl.ds(base + c * 128, 128), :] = src[pl.ds(c * per, per)].reshape(128, 128).astype(F32)

    def prepare(u):
        wt[u] = proj_w[u].astype(F32).T.astype(BF16)
        gains[0, u] = jnp.broadcast_to(norm_gain[u : u + 1, :], (128, 128)).T

    def prepare_late(u):
        gwt[u] = gate_w[u].astype(F32).T.astype(BF16)
        owt[u] = out_w[u].astype(F32).T.astype(BF16)
        gains[1, u] = jnp.broadcast_to(mix_gain[u : u + 1, :], (128, 128)).T

    def span(r):
        return slice(r * 512, r * 512 + 512)

    def norm_row(u, r):
        nt[:, span(r)] = (normalize(xt[:, span(r)]) * tiled(gains[0, u])).astype(BF16)

    def keep(u, r):
        own = mask[0, r].astype(F32)
        if u == 0:
            return own
        return own * jnp.concatenate([mrow[q : q + 1, :] for q in range(4)], axis=1)

    def panel(u, r, p):
        proj = jnp.dot(wt[u, p * 256 : p * 256 + 256, :], nt[:, span(r)], preferred_element_type=F32)
        return sigmoid(proj[:128]) * proj[128:] * keep(u, r)

    def finish(u, r, recv, k):
        arrived(k, recv)
        unpack(r * 512, 4, recv)
        tri = jnp.concatenate([flat[pl.ds(r * 512 + q, 128, stride=4), :] for q in range(4)], axis=1)
        normed = (normalize(tri) * tiled(gains[1, u])).astype(BF16)
        result = jnp.dot(owt[u], normed, preferred_element_type=F32)
        gate = sigmoid(jnp.dot(gwt[u], nt[:, span(r)], preferred_element_type=F32))
        return xt[:, span(r)] + gate * result

    def part(value, q):
        return value[:, q * 128 : q * 128 + 128]

    for load in loads[:3]:
        load.wait()
    prepare(0)
    for r in range(4):
        flat[pl.ds(r * 512, 512), :] = pair[r].astype(F32)
    for r in range(4):
        for q in range(4):
            at = (r * 4 + q) * 128
            xt[:, at : at + 128] = flat[pl.ds(r * 512 + q, 128, stride=4), :].T
    for r in range(4):
        norm_row(0, r)
        value = panel(0, r, 1)
        for q in range(4):
            flat[pl.ds(2048 + r * 4 + q, 128, stride=16), :] = part(value, q)
    pack(2048, 16, r0_send)

    lane = lax.broadcasted_iota(jnp.int32, (1, 128), 1)
    row = jnp.zeros((1, 128), F32)
    for r in range(4):
        row = jnp.where(lane == r, mask[0, r].astype(F32), row)
    msend[...] = row

    pl.semaphore_wait(barrier, ND - 1)
    exchange(R0, r0_send, r0_recv)
    for r in range(4):
        value = panel(0, r, 0)
        for q in range(4):
            flat[pl.ds(r * 512 + q, 128, stride=4), :] = part(value, q)
        pack(r * 512, 4, l0_send.at[r])
        exchange(L0 + r, l0_send.at[r], l0_recv.at[r])
        if r == 0:
            to_all(
                lambda peer: pltpu.make_async_remote_copy(
                    msend, mrecv.at[me], ssem.at[MASK], rsem.at[MASK], device_id=(peer,), device_id_type=MESH
                ).start()
            )
            mrecv[me] = msend[...]
    for load in loads[3:]:
        load.wait()
    prepare(1)
    prepare_late(0)
    prepare_late(1)

    arrived(MASK, mrecv)
    mrow[...] = mrecv[...].reshape(128, 128).T[0:8]
    arrived(R0, r0_recv)
    unpack(0, 16, r0_recv)
    for r in range(4):
        for q in range(4):
            block = flat[pl.ds(r * 4 + q, 128, stride=16), :]
            mat_b[r * 128 : r * 128 + 128, q * 128 : q * 128 + 128] = block.astype(BF16)
    for r in range(4):
        arrived(L0 + r, l0_recv.at[r])
        unpack(r * 512, 4, l0_recv.at[r])
        for q in range(4):
            block = flat[pl.ds(r * 512 + q, 128, stride=4), :] * mrow[q : q + 1, :]
            mat_a[r, :, q * 128 : q * 128 + 128] = block.astype(BF16)
        tri = lax.dot_general(mat_a[r], mat_b[...], (((1,), (1,)), ((), ())), preferred_element_type=F32)
        for q in range(4):
            flat[pl.ds(2048 + r * 512 + q, 128, stride=4), :] = part(tri, q)
        pack(2048 + r * 512, 4, t0_send.at[r])
        exchange(T0 + r, t0_send.at[r], t0_recv.at[r])

    for r in range(4):
        xt[:, span(r)] = finish(0, r, t0_recv.at[r], T0 + r).astype(BF16).astype(F32)
        norm_row(1, r)
        value = panel(1, r, 1)
        for q in range(4):
            flat[pl.ds(r * 512 + q, 128, stride=4), :] = part(value, q)
        pack(r * 512, 4, r1_send.at[r])
        exchange(R1 + r, r1_send.at[r], r1_recv.at[r])
        value = panel(1, r, 0)
        for q in range(4):
            flat[pl.ds(2048 + q * 512 + r, 128, stride=4), :] = part(value, q)
    for q in range(4):
        pack(2048 + q * 512, 4, l1_send.at[q])
        exchange(L1 + q, l1_send.at[q], l1_recv.at[q])

    for r in range(4):
        arrived(R1 + r, r1_recv.at[r])
        unpack(r * 512, 4, r1_recv.at[r])
        for q in range(4):
            block = flat[pl.ds(r * 512 + q, 128, stride=4), :]
            mat_b[r * 128 : r * 128 + 128, q * 128 : q * 128 + 128] = block.astype(BF16)
    for q in range(4):
        arrived(L1 + q, l1_recv.at[q])
        unpack(q * 512, 4, l1_recv.at[q])
        for r in range(4):
            block = flat[pl.ds(q * 512 + r, 128, stride=4), :]
            mat_a[q, :, r * 128 : r * 128 + 128] = block.T.astype(BF16)
        tri = jnp.dot(mat_a[q], mat_b[...], preferred_element_type=F32)
        for t in range(4):
            flat[pl.ds(2048 + q * 512 + t, 128, stride=4), :] = part(tri, t)
        pack(2048 + q * 512, 4, t1_send.at[q])
        exchange(T1 + q, t1_send.at[q], t1_recv.at[q])

    stores = []
    for r in range(4):
        value = finish(1, r, t1_recv.at[r], T1 + r)
        for q in range(4):
            flat[pl.ds(2048 + r * 512 + q, 128, stride=4), :] = part(value, q).T
        pair[r] = flat[pl.ds(2048 + r * 512, 512), :].astype(BF16)
        stores.append(pltpu.make_async_copy(pair.at[r], out_h.at[r], isem.at[r]))
        stores[-1].start()
    sent(MASK, mrecv)
    sent(R0, r0_send)
    for k, src in ((L0, l0_send), (T0, t0_send), (R1, r1_send), (L1, l1_send), (T1, t1_send)):
        for r in range(4):
            sent(k + r, src.at[r])
    for store in stores:
        store.wait()


def body(pair, residue_mask, norm_gain, proj_weight, gate_weight, mix_gain, out_weight):
    hbm = pl.BlockSpec(memory_space=pltpu.HBM)
    chunks = [pltpu.VMEM((4, ND, 4, 128), BF16)]
    return pl.pallas_call(
        kernel,
        out_shape=jax.ShapeDtypeStruct((4, 512, 128), BF16),
        in_specs=[hbm, pl.BlockSpec(memory_space=pltpu.SMEM)] + [hbm] * 5,
        out_specs=hbm,
        scratch_shapes=[
            pltpu.VMEM((4, 512, 128), BF16),
            pltpu.VMEM((2, 128), F32),
            pltpu.VMEM((2, 128, 512), BF16),
            pltpu.VMEM((2, 128, 128), BF16),
            pltpu.VMEM((2, 128), F32),
            pltpu.VMEM((2, 128, 128), BF16),
            pltpu.SemaphoreType.DMA((6,)),
            pltpu.VMEM((128, 2048), F32),
            pltpu.VMEM((128, 2048), BF16),
            pltpu.VMEM((2, 512, 128), BF16),
            pltpu.VMEM((2, 128, 128), BF16),
            pltpu.VMEM((2, 128, 128), BF16),
            pltpu.VMEM((2, 2, 128, 128), F32),
            pltpu.VMEM((4096, 128), F32),
            pltpu.VMEM((4, 128, 512), BF16),
            pltpu.VMEM((512, 512), BF16),
            pltpu.VMEM((1, 128), F32),
            pltpu.VMEM((ND, 1, 128), F32),
            pltpu.VMEM((8, 128), F32),
        ]
        + [pltpu.VMEM((ND, 16, 128), BF16)] * 2
        + chunks * 10
        + [pltpu.SemaphoreType.DMA((KINDS,))] * 2,
        compiler_params=pltpu.CompilerParams(
            collective_id=0, has_side_effects=True, vmem_limit_bytes=67_043_328
        ),
    )(pair, residue_mask.reshape(1, 4), norm_gain, proj_weight, gate_weight, mix_gain, out_weight)


def solution(mesh):
    in_specs = (P("dap", None, None), P("dap"), P(), P(), P(), P(), P())
    return jax.shard_map(body, mesh=mesh, in_specs=in_specs, out_specs=P("dap", None, None), check_vma=False)
```

time: 67.8 us -> 58.8 us (0.87)
  Pallas kernels: 65.8 us -> 56.8 us
    pallas_call x1, Pallas kernels: 65.8 us -> 56.8 us  [body(): pl.pallas_call(kernel, out_shape=jax.ShapeDtypeStruct((4, 512, 128), BF16...]
where the time goes in v2:
time: 58.8 us; the launch traced here: 58.7 us
  Pallas kernels  56.8 us (97%)
  local copies, waits for them, and re-layouts  1.87 us (3%)
    pallas_call x1, Pallas kernels, body(): pl.pallas_call(kernel, out_shape=jax.ShapeDtypeStruct((4, 512, 128), BF16...  56.8 us
    unnamed x1, local copies, waits for them, and re-layouts  1.87 us

profile of v2, /device:TPU:1, one launch (start us, length us, event | category | flops | bytes accessed | tf_op | source)
XLA Modules:
  0.0 58.7 jit_solution(16712085350120150300)
XLA Ops:
  0.0 56.8 %shard_map.73 = bf16[4,512,128]{2,1,0:T(8,128)(2,1)} custom-call(bf16[4,512,128]{2,1,0:T(8,128)(2,1)} %pair_h.1, s32[1,4]{1,0:T(1,128)} %bitcast.1, f32[2,128]{1,0:T(2,128)} %norm_gain_h.1, bf16[2,128,512]{2,1,0:T(8,128)(2,1)} %proj_w_h.1, bf16[2,128,128]{2,1,0:T(8,128)(2,1)} %gate_w_h.1, f32[2,128]{1,0:T(2,128)} %mix_gain_h.1, bf16[2,128,128]{2,1,0:T(8,128)(2,1)} %out_w_h.1), custom_call_target="tpu_custom_call" | custom-call | tf_op jit(solution)/shard_map/pallas_call | solution.py:254
  56.8 1.9 %copy.9 = bf16[4,512,128]{2,1,0:T(8,128)(2,1)} copy(bf16[4,512,128]{2,1,0:T(8,128)(2,1)} %shard_map.73) | data formatting | bytes 1048576

commit v3 on v2

--- a/solution.py
+++ b/solution.py
@@ -10,7 +10,8 @@
 MESH = pl.DeviceIdType.MESH
 F32 = jnp.float32
 BF16 = jnp.bfloat16
-R0, L0, T0, R1, L1, T1, MASK, KINDS = 0, 1, 5, 9, 13, 17, 21, 22
+R0, L0, T0, R1, L1, T1, KINDS = 0, 1, 5, 9, 11, 15, 19
+MASKED = 2.0**100
 
 
 def sigmoid(v):
@@ -43,14 +44,14 @@
 
 
 def kernel(
-    pair_h, mask, norm_gain_h, proj_w_h, gate_w_h, mix_gain_h, out_w_h, out_h,
-    pair, norm_gain, proj_w, gate_w, mix_gain, out_w, isem,
-    xt, nt, wt, gwt, owt, gains, flat, mat_a, mat_b, msend, mrecv, mrow,
+    pair_h, mask_h, norm_gain_h, proj_w_h, gate_w_h, mix_gain_h, out_w_h, out,
+    pair, mask, norm_gain, proj_w, gate_w, mix_gain, out_w, isem,
+    xt, nt, wt, gwt, owt, gains, flat, mat_a, mat_b, mrow,
     r0_send, r0_recv, l0_send, l0_recv, t0_send, t0_recv, r1_send, r1_recv, l1_send, l1_recv, t1_send, t1_recv,
     ssem, rsem,
 ):
     pairs = (
-        (pair_h, pair), (proj_w_h, proj_w), (norm_gain_h, norm_gain),
+        (pair_h, pair), (proj_w_h, proj_w), (norm_gain_h, norm_gain), (mask_h, mask),
         (gate_w_h, gate_w), (mix_gain_h, mix_gain), (out_w_h, out_w),
     )
     loads = [pltpu.make_async_copy(a, b, isem.at[i]) for i, (a, b) in enumerate(pairs)]
@@ -121,7 +122,10 @@
 
     def panel(u, r, p):
         proj = jnp.dot(wt[u, p * 256 : p * 256 + 256, :], nt[:, span(r)], preferred_element_type=F32)
-        return sigmoid(proj[:128]) * proj[128:] * keep(u, r)
+        value = sigmoid(proj[:128]) * proj[128:] * keep(u, r)
+        if u == 0 and p == 1:
+            value = value + (1.0 - mask[0, r].astype(F32)) * MASKED
+        return value
 
     def finish(u, r, recv, k):
         arrived(k, recv)
@@ -135,7 +139,7 @@
     def part(value, q):
         return value[:, q * 128 : q * 128 + 128]
 
-    for load in loads[:3]:
+    for load in loads[:4]:
         load.wait()
     prepare(0)
     for r in range(4):
@@ -150,12 +154,6 @@
         for q in range(4):
             flat[pl.ds(2048 + r * 4 + q, 128, stride=16), :] = part(value, q)
     pack(2048, 16, r0_send)
-
-    lane = lax.broadcasted_iota(jnp.int32, (1, 128), 1)
-    row = jnp.zeros((1, 128), F32)
-    for r in range(4):
-        row = jnp.where(lane == r, mask[0, r].astype(F32), row)
-    msend[...] = row
 
     pl.semaphore_wait(barrier, ND - 1)
     exchange(R0, r0_send, r0_recv)
@@ -165,26 +163,20 @@
             flat[pl.ds(r * 512 + q, 128, stride=4), :] = part(value, q)
         pack(r * 512, 4, l0_send.at[r])
         exchange(L0 + r, l0_send.at[r], l0_recv.at[r])
-        if r == 0:
-            to_all(
-                lambda peer: pltpu.make_async_remote_copy(
-                    msend, mrecv.at[me], ssem.at[MASK], rsem.at[MASK], device_id=(peer,), device_id_type=MESH
-                ).start()
-            )
-            mrecv[me] = msend[...]
-    for load in loads[3:]:
+    for load in loads[4:]:
         load.wait()
     prepare(1)
     prepare_late(0)
     prepare_late(1)
 
-    arrived(MASK, mrecv)
-    mrow[...] = mrecv[...].reshape(128, 128).T[0:8]
     arrived(R0, r0_recv)
     unpack(0, 16, r0_recv)
     for r in range(4):
         for q in range(4):
             block = flat[pl.ds(r * 4 + q, 128, stride=16), :]
+            if q == 0:
+                mrow[r : r + 1, :] = jnp.where(block.T[0:1] > 0.5 * MASKED, 0.0, 1.0)
+            block = jnp.where(block > 0.5 * MASKED, 0.0, block)
             mat_b[r * 128 : r * 128 + 128, q * 128 : q * 128 + 128] = block.astype(BF16)
     for r in range(4):
         arrived(L0 + r, l0_recv.at[r])
@@ -198,27 +190,30 @@
         pack(2048 + r * 512, 4, t0_send.at[r])
         exchange(T0 + r, t0_send.at[r], t0_recv.at[r])
 
-    for r in range(4):
-        xt[:, span(r)] = finish(0, r, t0_recv.at[r], T0 + r).astype(BF16).astype(F32)
-        norm_row(1, r)
-        value = panel(1, r, 1)
-        for q in range(4):
-            flat[pl.ds(r * 512 + q, 128, stride=4), :] = part(value, q)
-        pack(r * 512, 4, r1_send.at[r])
-        exchange(R1 + r, r1_send.at[r], r1_recv.at[r])
-        value = panel(1, r, 0)
-        for q in range(4):
-            flat[pl.ds(2048 + q * 512 + r, 128, stride=4), :] = part(value, q)
+    for g in range(2):
+        for r in (2 * g, 2 * g + 1):
+            xt[:, span(r)] = finish(0, r, t0_recv.at[r], T0 + r).astype(BF16).astype(F32)
+            norm_row(1, r)
+            value = panel(1, r, 1)
+            for q in range(4):
+                flat[pl.ds(4096 + g * 1024 + (r - 2 * g) * 4 + q, 128, stride=8), :] = part(value, q)
+        pack(4096 + g * 1024, 8, r1_send.at[g])
+        exchange(R1 + g, r1_send.at[g], r1_recv.at[g])
+        for r in (2 * g, 2 * g + 1):
+            value = panel(1, r, 0)
+            for q in range(4):
+                flat[pl.ds(2048 + q * 512 + r, 128, stride=4), :] = part(value, q)
     for q in range(4):
         pack(2048 + q * 512, 4, l1_send.at[q])
         exchange(L1 + q, l1_send.at[q], l1_recv.at[q])
 
-    for r in range(4):
-        arrived(R1 + r, r1_recv.at[r])
-        unpack(r * 512, 4, r1_recv.at[r])
-        for q in range(4):
-            block = flat[pl.ds(r * 512 + q, 128, stride=4), :]
-            mat_b[r * 128 : r * 128 + 128, q * 128 : q * 128 + 128] = block.astype(BF16)
+    for g in range(2):
+        arrived(R1 + g, r1_recv.at[g])
+        unpack(g * 1024, 8, r1_recv.at[g])
+        for r in (2 * g, 2 * g + 1):
+            for q in range(4):
+                block = flat[pl.ds(g * 1024 + (r - 2 * g) * 4 + q, 128, stride=8), :]
+                mat_b[r * 128 : r * 128 + 128, q * 128 : q * 128 + 128] = block.astype(BF16)
     for q in range(4):
         arrived(L1 + q, l1_recv.at[q])
         unpack(q * 512, 4, l1_recv.at[q])
@@ -231,59 +226,58 @@
         pack(2048 + q * 512, 4, t1_send.at[q])
         exchange(T1 + q, t1_send.at[q], t1_recv.at[q])
 
-    stores = []
     for r in range(4):
         value = finish(1, r, t1_recv.at[r], T1 + r)
         for q in range(4):
             flat[pl.ds(2048 + r * 512 + q, 128, stride=4), :] = part(value, q).T
-        pair[r] = flat[pl.ds(2048 + r * 512, 512), :].astype(BF16)
-        stores.append(pltpu.make_async_copy(pair.at[r], out_h.at[r], isem.at[r]))
-        stores[-1].start()
-    sent(MASK, mrecv)
+        out[r] = flat[pl.ds(2048 + r * 512, 512), :].astype(BF16)
     sent(R0, r0_send)
-    for k, src in ((L0, l0_send), (T0, t0_send), (R1, r1_send), (L1, l1_send), (T1, t1_send)):
-        for r in range(4):
+    for k, src, parts in ((L0, l0_send, 4), (T0, t0_send, 4), (R1, r1_send, 2), (L1, l1_send, 4), (T1, t1_send, 4)):
+        for r in range(parts):
             sent(k + r, src.at[r])
-    for store in stores:
-        store.wait()
-
-
-def body(pair, residue_mask, norm_gain, proj_weight, gate_weight, mix_gain, out_weight):
+
+
+def at_hbm(a):
+    return pltpu.with_memory_space_constraint(a, pltpu.HBM)
+
+
+def body(*args):
     hbm = pl.BlockSpec(memory_space=pltpu.HBM)
     chunks = [pltpu.VMEM((4, ND, 4, 128), BF16)]
     return pl.pallas_call(
         kernel,
-        out_shape=jax.ShapeDtypeStruct((4, 512, 128), BF16),
-        in_specs=[hbm, pl.BlockSpec(memory_space=pltpu.SMEM)] + [hbm] * 5,
-        out_specs=hbm,
+        out_shape=pltpu.VMEM((4, 512, 128), BF16),
+        in_specs=[hbm] * 7,
+        out_specs=pl.BlockSpec(memory_space=pltpu.VMEM),
         scratch_shapes=[
             pltpu.VMEM((4, 512, 128), BF16),
+            pltpu.SMEM((1, 4), jnp.int32),
             pltpu.VMEM((2, 128), F32),
             pltpu.VMEM((2, 128, 512), BF16),
             pltpu.VMEM((2, 128, 128), BF16),
             pltpu.VMEM((2, 128), F32),
             pltpu.VMEM((2, 128, 128), BF16),
-            pltpu.SemaphoreType.DMA((6,)),
+            pltpu.SemaphoreType.DMA((7,)),
             pltpu.VMEM((128, 2048), F32),
             pltpu.VMEM((128, 2048), BF16),
             pltpu.VMEM((2, 512, 128), BF16),
             pltpu.VMEM((2, 128, 128), BF16),
             pltpu.VMEM((2, 128, 128), BF16),
             pltpu.VMEM((2, 2, 128, 128), F32),
-            pltpu.VMEM((4096, 128), F32),
+            pltpu.VMEM((6144, 128), F32),
             pltpu.VMEM((4, 128, 512), BF16),
             pltpu.VMEM((512, 512), BF16),
-            pltpu.VMEM((1, 128), F32),
-            pltpu.VMEM((ND, 1, 128), F32),
             pltpu.VMEM((8, 128), F32),
         ]
         + [pltpu.VMEM((ND, 16, 128), BF16)] * 2
-        + chunks * 10
+        + chunks * 4
+        + [pltpu.VMEM((2, ND, 8, 128), BF16)] * 2
+        + chunks * 4
         + [pltpu.SemaphoreType.DMA((KINDS,))] * 2,
         compiler_params=pltpu.CompilerParams(
-            collective_id=0, has_side_effects=True, vmem_limit_bytes=67_043_328
+            collective_id=0, has_side_effects=True, vmem_limit_bytes=48 << 20
         ),
-    )(pair, residue_mask.reshape(1, 4), norm_gain, proj_weight, gate_weight, mix_gain, out_weight)
+    )(*(at_hbm(a if a.ndim > 1 else a.reshape(1, 4)) for a in args))
 
 
 def solution(mesh):

time: 58.8 us -> 54.8 us (0.932)
  Pallas kernels: 56.8 us -> 53.9 us
  local copies, waits for them, and re-layouts: 1.87 us -> 0.8 us
    pallas_call x1, Pallas kernels: 56.8 us -> 53.9 us  [body(): pl.pallas_call(kernel, out_shape=pltpu.VMEM((4, 512, 128), BF16), in_spec...]
    unnamed x1, local copies, waits for them, and re-layouts: 1.87 us -> 0.8 us
where the time goes in v3:
time: 54.8 us; the launch traced here: 54.7 us
  Pallas kernels  53.9 us (98%)
  local copies, waits for them, and re-layouts  0.8 us (1%)
    pallas_call x1, Pallas kernels, body(): pl.pallas_call(kernel, out_shape=pltpu.VMEM((4, 512, 128), BF16), in_spec...  53.9 us

profile of v3, /device:TPU:1, one launch (start us, length us, event | category | flops | bytes accessed | tf_op | source)
XLA Modules:
  0.0 54.7 jit_solution(12024559963385525552)
XLA Ops:
  0.0 53.9 %shard_map.73 = bf16[4,512,128]{2,1,0:T(8,128)(2,1)S(1)} custom-call(bf16[4,512,128]{2,1,0:T(8,128)(2,1)} %pair_h.1, s32[1,4]{1,0:T(1,128)} %bitcast.1, f32[2,128]{1,0:T(2,128)} %norm_gain_h.1, bf16[2,128,512]{2,1,0:T(8,128)(2,1)} %proj_w_h.1, bf16[2,128,128]{2,1,0:T(8,128)(2,1)} %gate_w_h.1, f32[2,128]{1,0:T(2,128)} %mix_gain_h.1, bf16[2,128,128]{2,1,0:T(8,128)(2,1)} %out_w_h.1), custom_call_target="tpu_custom_call" | custom-call | tf_op jit(solution)/shard_map/pallas_call | solution.py:247
  53.9 0.8 %copy.9 = bf16[4,512,128]{2,1,0:T(8,128)(2,1)} copy(bf16[4,512,128]{2,1,0:T(8,128)(2,1)S(1)} %shard_map.73) | data formatting | bytes 1048576

commit v4 on v3

--- a/solution.py
+++ b/solution.py
@@ -10,7 +10,8 @@
 MESH = pl.DeviceIdType.MESH
 F32 = jnp.float32
 BF16 = jnp.bfloat16
-R0, L0, T0, R1, L1, T1, KINDS = 0, 1, 5, 9, 11, 15, 19
+R0, L0, T0, R1, L1, T1, KINDS = 0, 2, 6, 10, 14, 18, 22
+R1_ROWS = ((0,), (1,), (2,), (3,))
 MASKED = 2.0**100
 
 
@@ -46,8 +47,8 @@
 def kernel(
     pair_h, mask_h, norm_gain_h, proj_w_h, gate_w_h, mix_gain_h, out_w_h, out,
     pair, mask, norm_gain, proj_w, gate_w, mix_gain, out_w, isem,
-    xt, nt, wt, gwt, owt, gains, flat, mat_a, mat_b, mrow,
-    r0_send, r0_recv, l0_send, l0_recv, t0_send, t0_recv, r1_send, r1_recv, l1_send, l1_recv, t1_send, t1_recv,
+    xt, nt, gates, wt, gwt, owt, gains, flat, mat_a, mat_b, mrow,
+    r0_send, r0_recv, l0_send, l0_recv, t0_send, t0_recv, r1_send, r1_recv, r1_send2, r1_recv2, l1_send, l1_recv, t1_send, t1_recv,
     ssem, rsem,
 ):
     pairs = (
@@ -133,8 +134,10 @@
         tri = jnp.concatenate([flat[pl.ds(r * 512 + q, 128, stride=4), :] for q in range(4)], axis=1)
         normed = (normalize(tri) * tiled(gains[1, u])).astype(BF16)
         result = jnp.dot(owt[u], normed, preferred_element_type=F32)
-        gate = sigmoid(jnp.dot(gwt[u], nt[:, span(r)], preferred_element_type=F32))
-        return xt[:, span(r)] + gate * result
+        return xt[:, span(r)] + gates[:, span(r)] * result
+
+    def gate_row(u, r):
+        gates[:, span(r)] = sigmoid(jnp.dot(gwt[u], nt[:, span(r)], preferred_element_type=F32))
 
     def part(value, q):
         return value[:, q * 128 : q * 128 + 128]
@@ -148,15 +151,16 @@
         for q in range(4):
             at = (r * 4 + q) * 128
             xt[:, at : at + 128] = flat[pl.ds(r * 512 + q, 128, stride=4), :].T
-    for r in range(4):
-        norm_row(0, r)
-        value = panel(0, r, 1)
-        for q in range(4):
-            flat[pl.ds(2048 + r * 4 + q, 128, stride=16), :] = part(value, q)
-    pack(2048, 16, r0_send)
-
-    pl.semaphore_wait(barrier, ND - 1)
-    exchange(R0, r0_send, r0_recv)
+    for g in range(2):
+        for r in (2 * g, 2 * g + 1):
+            norm_row(0, r)
+            value = panel(0, r, 1)
+            for q in range(4):
+                flat[pl.ds(2048 + g * 1024 + (r - 2 * g) * 4 + q, 128, stride=8), :] = part(value, q)
+        pack(2048 + g * 1024, 8, r0_send.at[g])
+        if g == 0:
+            pl.semaphore_wait(barrier, ND - 1)
+        exchange(R0 + g, r0_send.at[g], r0_recv.at[g])
     for r in range(4):
         value = panel(0, r, 0)
         for q in range(4):
@@ -168,16 +172,19 @@
     prepare(1)
     prepare_late(0)
     prepare_late(1)
-
-    arrived(R0, r0_recv)
-    unpack(0, 16, r0_recv)
-    for r in range(4):
-        for q in range(4):
-            block = flat[pl.ds(r * 4 + q, 128, stride=16), :]
-            if q == 0:
-                mrow[r : r + 1, :] = jnp.where(block.T[0:1] > 0.5 * MASKED, 0.0, 1.0)
-            block = jnp.where(block > 0.5 * MASKED, 0.0, block)
-            mat_b[r * 128 : r * 128 + 128, q * 128 : q * 128 + 128] = block.astype(BF16)
+    for r in range(4):
+        gate_row(0, r)
+
+    for g in range(2):
+        arrived(R0 + g, r0_recv.at[g])
+        unpack(g * 1024, 8, r0_recv.at[g])
+        for r in (2 * g, 2 * g + 1):
+            for q in range(4):
+                block = flat[pl.ds(g * 1024 + (r - 2 * g) * 4 + q, 128, stride=8), :]
+                if q == 0:
+                    mrow[r : r + 1, :] = jnp.where(block.T[0:1] > 0.5 * MASKED, 0.0, 1.0)
+                block = jnp.where(block > 0.5 * MASKED, 0.0, block)
+                mat_b[r * 128 : r * 128 + 128, q * 128 : q * 128 + 128] = block.astype(BF16)
     for r in range(4):
         arrived(L0 + r, l0_recv.at[r])
         unpack(r * 512, 4, l0_recv.at[r])
@@ -190,29 +197,38 @@
         pack(2048 + r * 512, 4, t0_send.at[r])
         exchange(T0 + r, t0_send.at[r], t0_recv.at[r])
 
-    for g in range(2):
-        for r in (2 * g, 2 * g + 1):
+    def left_row(r):
+        value = panel(1, r, 0)
+        for q in range(4):
+            flat[pl.ds(2048 + q * 512 + r, 128, stride=4), :] = part(value, q)
+
+    r1 = [(r1_send.at[i], r1_recv.at[i]) if len(rows) == 1 else (r1_send2, r1_recv2) for i, rows in enumerate(R1_ROWS)]
+    for i, rows in enumerate(R1_ROWS):
+        n = len(rows)
+        for r in rows:
             xt[:, span(r)] = finish(0, r, t0_recv.at[r], T0 + r).astype(BF16).astype(F32)
             norm_row(1, r)
             value = panel(1, r, 1)
             for q in range(4):
-                flat[pl.ds(4096 + g * 1024 + (r - 2 * g) * 4 + q, 128, stride=8), :] = part(value, q)
-        pack(4096 + g * 1024, 8, r1_send.at[g])
-        exchange(R1 + g, r1_send.at[g], r1_recv.at[g])
-        for r in (2 * g, 2 * g + 1):
-            value = panel(1, r, 0)
-            for q in range(4):
-                flat[pl.ds(2048 + q * 512 + r, 128, stride=4), :] = part(value, q)
+                flat[pl.ds(4096 + rows[0] * 512 + (r - rows[0]) * 4 + q, 128, stride=4 * n), :] = part(value, q)
+        pack(4096 + rows[0] * 512, 4 * n, r1[i][0])
+        exchange(R1 + i, *r1[i])
+    for r in range(4):
+        left_row(r)
     for q in range(4):
         pack(2048 + q * 512, 4, l1_send.at[q])
         exchange(L1 + q, l1_send.at[q], l1_recv.at[q])
 
-    for g in range(2):
-        arrived(R1 + g, r1_recv.at[g])
-        unpack(g * 1024, 8, r1_recv.at[g])
-        for r in (2 * g, 2 * g + 1):
+    for r in range(4):
+        gate_row(1, r)
+
+    for i, rows in enumerate(R1_ROWS):
+        n = len(rows)
+        arrived(R1 + i, r1[i][1])
+        unpack(rows[0] * 512, 4 * n, r1[i][1])
+        for r in rows:
             for q in range(4):
-                block = flat[pl.ds(g * 1024 + (r - 2 * g) * 4 + q, 128, stride=8), :]
+                block = flat[pl.ds(rows[0] * 512 + (r - rows[0]) * 4 + q, 128, stride=4 * n), :]
                 mat_b[r * 128 : r * 128 + 128, q * 128 : q * 128 + 128] = block.astype(BF16)
     for q in range(4):
         arrived(L1 + q, l1_recv.at[q])
@@ -231,8 +247,15 @@
         for q in range(4):
             flat[pl.ds(2048 + r * 512 + q, 128, stride=4), :] = part(value, q).T
         out[r] = flat[pl.ds(2048 + r * 512, 512), :].astype(BF16)
-    sent(R0, r0_send)
-    for k, src, parts in ((L0, l0_send, 4), (T0, t0_send, 4), (R1, r1_send, 2), (L1, l1_send, 4), (T1, t1_send, 4)):
+    for i in range(len(R1_ROWS)):
+        sent(R1 + i, r1[i][0])
+    for k, src, parts in (
+        (R0, r0_send, 2),
+        (L0, l0_send, 4),
+        (T0, t0_send, 4),
+        (L1, l1_send, 4),
+        (T1, t1_send, 4),
+    ):
         for r in range(parts):
             sent(k + r, src.at[r])
 
@@ -260,6 +283,7 @@
             pltpu.SemaphoreType.DMA((7,)),
             pltpu.VMEM((128, 2048), F32),
             pltpu.VMEM((128, 2048), BF16),
+            pltpu.VMEM((128, 2048), F32),
             pltpu.VMEM((2, 512, 128), BF16),
             pltpu.VMEM((2, 128, 128), BF16),
             pltpu.VMEM((2, 128, 128), BF16),
@@ -269,9 +293,9 @@
             pltpu.VMEM((512, 512), BF16),
             pltpu.VMEM((8, 128), F32),
         ]
-        + [pltpu.VMEM((ND, 16, 128), BF16)] * 2
-        + chunks * 4
         + [pltpu.VMEM((2, ND, 8, 128), BF16)] * 2
+        + chunks * 6
+        + [pltpu.VMEM((ND, 8, 128), BF16)] * 2
         + chunks * 4
         + [pltpu.SemaphoreType.DMA((KINDS,))] * 2,
         compiler_params=pltpu.CompilerParams(

time: 54.8 us -> 54.1 us (0.987)
  Pallas kernels: 53.9 us -> 53.2 us
    pallas_call x1, Pallas kernels: 53.9 us -> 53.2 us  [body(): pl.pallas_call(kernel, out_shape=pltpu.VMEM((4, 512, 128), BF16), in_spec...]
where the time goes in v4:
time: 54.1 us; the launch traced here: 54 us
  Pallas kernels  53.2 us (98%)
  local copies, waits for them, and re-layouts  0.8 us (1%)
    pallas_call x1, Pallas kernels, body(): pl.pallas_call(kernel, out_shape=pltpu.VMEM((4, 512, 128), BF16), in_spec...  53.2 us

profile of v4, /device:TPU:1, one launch (start us, length us, event | category | flops | bytes accessed | tf_op | source)
XLA Modules:
  0.0 54.0 jit_solution(471302113831254024)
XLA Ops:
  0.0 53.2 %shard_map.73 = bf16[4,512,128]{2,1,0:T(8,128)(2,1)S(1)} custom-call(bf16[4,512,128]{2,1,0:T(8,128)(2,1)} %pair_h.1, s32[1,4]{1,0:T(1,128)} %bitcast.1, f32[2,128]{1,0:T(2,128)} %norm_gain_h.1, bf16[2,128,512]{2,1,0:T(8,128)(2,1)} %proj_w_h.1, bf16[2,128,128]{2,1,0:T(8,128)(2,1)} %gate_w_h.1, f32[2,128]{1,0:T(2,128)} %mix_gain_h.1, bf16[2,128,128]{2,1,0:T(8,128)(2,1)} %out_w_h.1), custom_call_target="tpu_custom_call" | custom-call | tf_op jit(solution)/shard_map/pallas_call | solution.py:270
  53.2 0.8 %copy.9 = bf16[4,512,128]{2,1,0:T(8,128)(2,1)} copy(bf16[4,512,128]{2,1,0:T(8,128)(2,1)S(1)} %shard_map.73) | data formatting | bytes 1048576

commit v5 on v4

--- a/solution.py
+++ b/solution.py
@@ -10,8 +10,7 @@
 MESH = pl.DeviceIdType.MESH
 F32 = jnp.float32
 BF16 = jnp.bfloat16
-R0, L0, T0, R1, L1, T1, KINDS = 0, 2, 6, 10, 14, 18, 22
-R1_ROWS = ((0,), (1,), (2,), (3,))
+R0, L0, T0, R1, L1, T1, KINDS = 0, 4, 8, 12, 16, 20, 24
 MASKED = 2.0**100
 
 
@@ -48,7 +47,7 @@
     pair_h, mask_h, norm_gain_h, proj_w_h, gate_w_h, mix_gain_h, out_w_h, out,
     pair, mask, norm_gain, proj_w, gate_w, mix_gain, out_w, isem,
     xt, nt, gates, wt, gwt, owt, gains, flat, mat_a, mat_b, mrow,
-    r0_send, r0_recv, l0_send, l0_recv, t0_send, t0_recv, r1_send, r1_recv, r1_send2, r1_recv2, l1_send, l1_recv, t1_send, t1_recv,
+    r0_send, r0_recv, l0_send, l0_recv, t0_send, t0_recv, r1_send, r1_recv, l1_send, l1_recv, t1_send, t1_recv,
     ssem, rsem,
 ):
     pairs = (
@@ -151,16 +150,15 @@
         for q in range(4):
             at = (r * 4 + q) * 128
             xt[:, at : at + 128] = flat[pl.ds(r * 512 + q, 128, stride=4), :].T
-    for g in range(2):
-        for r in (2 * g, 2 * g + 1):
-            norm_row(0, r)
-            value = panel(0, r, 1)
-            for q in range(4):
-                flat[pl.ds(2048 + g * 1024 + (r - 2 * g) * 4 + q, 128, stride=8), :] = part(value, q)
-        pack(2048 + g * 1024, 8, r0_send.at[g])
-        if g == 0:
+    for r in range(4):
+        norm_row(0, r)
+        value = panel(0, r, 1)
+        for q in range(4):
+            flat[pl.ds(2048 + r * 512 + q, 128, stride=4), :] = part(value, q)
+        pack(2048 + r * 512, 4, r0_send.at[r])
+        if r == 0:
             pl.semaphore_wait(barrier, ND - 1)
-        exchange(R0 + g, r0_send.at[g], r0_recv.at[g])
+        exchange(R0 + r, r0_send.at[r], r0_recv.at[r])
     for r in range(4):
         value = panel(0, r, 0)
         for q in range(4):
@@ -175,16 +173,15 @@
     for r in range(4):
         gate_row(0, r)
 
-    for g in range(2):
-        arrived(R0 + g, r0_recv.at[g])
-        unpack(g * 1024, 8, r0_recv.at[g])
-        for r in (2 * g, 2 * g + 1):
-            for q in range(4):
-                block = flat[pl.ds(g * 1024 + (r - 2 * g) * 4 + q, 128, stride=8), :]
-                if q == 0:
-                    mrow[r : r + 1, :] = jnp.where(block.T[0:1] > 0.5 * MASKED, 0.0, 1.0)
-                block = jnp.where(block > 0.5 * MASKED, 0.0, block)
-                mat_b[r * 128 : r * 128 + 128, q * 128 : q * 128 + 128] = block.astype(BF16)
+    for r in range(4):
+        arrived(R0 + r, r0_recv.at[r])
+        unpack(r * 512, 4, r0_recv.at[r])
+        for q in range(4):
+            block = flat[pl.ds(r * 512 + q, 128, stride=4), :]
+            if q == 0:
+                mrow[r : r + 1, :] = jnp.where(block.T[0:1] > 0.5 * MASKED, 0.0, 1.0)
+            block = jnp.where(block > 0.5 * MASKED, 0.0, block)
+            mat_b[r * 128 : r * 128 + 128, q * 128 : q * 128 + 128] = block.astype(BF16)
     for r in range(4):
         arrived(L0 + r, l0_recv.at[r])
         unpack(r * 512, 4, l0_recv.at[r])
@@ -202,17 +199,14 @@
         for q in range(4):
             flat[pl.ds(2048 + q * 512 + r, 128, stride=4), :] = part(value, q)
 
-    r1 = [(r1_send.at[i], r1_recv.at[i]) if len(rows) == 1 else (r1_send2, r1_recv2) for i, rows in enumerate(R1_ROWS)]
-    for i, rows in enumerate(R1_ROWS):
-        n = len(rows)
-        for r in rows:
-            xt[:, span(r)] = finish(0, r, t0_recv.at[r], T0 + r).astype(BF16).astype(F32)
-            norm_row(1, r)
-            value = panel(1, r, 1)
-            for q in range(4):
-                flat[pl.ds(4096 + rows[0] * 512 + (r - rows[0]) * 4 + q, 128, stride=4 * n), :] = part(value, q)
-        pack(4096 + rows[0] * 512, 4 * n, r1[i][0])
-        exchange(R1 + i, *r1[i])
+    for r in range(4):
+        xt[:, span(r)] = finish(0, r, t0_recv.at[r], T0 + r).astype(BF16).astype(F32)
+        norm_row(1, r)
+        value = panel(1, r, 1)
+        for q in range(4):
+            flat[pl.ds(4096 + r * 512 + q, 128, stride=4), :] = part(value, q)
+        pack(4096 + r * 512, 4, r1_send.at[r])
+        exchange(R1 + r, r1_send.at[r], r1_recv.at[r])
     for r in range(4):
         left_row(r)
     for q in range(4):
@@ -222,14 +216,12 @@
     for r in range(4):
         gate_row(1, r)
 
-    for i, rows in enumerate(R1_ROWS):
-        n = len(rows)
-        arrived(R1 + i, r1[i][1])
-        unpack(rows[0] * 512, 4 * n, r1[i][1])
-        for r in rows:
-            for q in range(4):
-                block = flat[pl.ds(rows[0] * 512 + (r - rows[0]) * 4 + q, 128, stride=4 * n), :]
-                mat_b[r * 128 : r * 128 + 128, q * 128 : q * 128 + 128] = block.astype(BF16)
+    for r in range(4):
+        arrived(R1 + r, r1_recv.at[r])
+        unpack(r * 512, 4, r1_recv.at[r])
+        for q in range(4):
+            block = flat[pl.ds(r * 512 + q, 128, stride=4), :]
+            mat_b[r * 128 : r * 128 + 128, q * 128 : q * 128 + 128] = block.astype(BF16)
     for q in range(4):
         arrived(L1 + q, l1_recv.at[q])
         unpack(q * 512, 4, l1_recv.at[q])
@@ -247,12 +239,11 @@
         for q in range(4):
             flat[pl.ds(2048 + r * 512 + q, 128, stride=4), :] = part(value, q).T
         out[r] = flat[pl.ds(2048 + r * 512, 512), :].astype(BF16)
-    for i in range(len(R1_ROWS)):
-        sent(R1 + i, r1[i][0])
     for k, src, parts in (
-        (R0, r0_send, 2),
+        (R0, r0_send, 4),
         (L0, l0_send, 4),
         (T0, t0_send, 4),
+        (R1, r1_send, 4),
         (L1, l1_send, 4),
         (T1, t1_send, 4),
     ):
@@ -288,15 +279,12 @@
             pltpu.VMEM((2, 128, 128), BF16),
             pltpu.VMEM((2, 128, 128), BF16),
             pltpu.VMEM((2, 2, 128, 128), F32),
-            pltpu.VMEM((6144, 128), F32),
+            pltpu.VMEM((6160, 128), F32),
             pltpu.VMEM((4, 128, 512), BF16),
             pltpu.VMEM((512, 512), BF16),
             pltpu.VMEM((8, 128), F32),
         ]
-        + [pltpu.VMEM((2, ND, 8, 128), BF16)] * 2
-        + chunks * 6
-        + [pltpu.VMEM((ND, 8, 128), BF16)] * 2
-        + chunks * 4
+        + chunks * 12
         + [pltpu.SemaphoreType.DMA((KINDS,))] * 2,
         compiler_params=pltpu.CompilerParams(
             collective_id=0, has_side_effects=True, vmem_limit_bytes=48 << 20

time: 54.1 us -> 54 us (level)
  no operation moved by 1% of the time
where the time goes in v5:
time: 54 us; the launch traced here: 53.9 us
  Pallas kernels  53.1 us (98%)
  local copies, waits for them, and re-layouts  0.8 us (1%)
    pallas_call x1, Pallas kernels, body(): pl.pallas_call(kernel, out_shape=pltpu.VMEM((4, 512, 128), BF16), in_spec...  53.1 us

profile of v5, /device:TPU:1, one launch (start us, length us, event | category | flops | bytes accessed | tf_op | source)
XLA Modules:
  0.0 53.9 jit_solution(17655623271658778463)
XLA Ops:
  0.0 53.1 %shard_map.73 = bf16[4,512,128]{2,1,0:T(8,128)(2,1)S(1)} custom-call(bf16[4,512,128]{2,1,0:T(8,128)(2,1)} %pair_h.1, s32[1,4]{1,0:T(1,128)} %bitcast.1, f32[2,128]{1,0:T(2,128)} %norm_gain_h.1, bf16[2,128,512]{2,1,0:T(8,128)(2,1)} %proj_w_h.1, bf16[2,128,128]{2,1,0:T(8,128)(2,1)} %gate_w_h.1, f32[2,128]{1,0:T(2,128)} %mix_gain_h.1, bf16[2,128,128]{2,1,0:T(8,128)(2,1)} %out_w_h.1), custom_call_target="tpu_custom_call" | custom-call | tf_op jit(solution)/shard_map/pallas_call | solution.py:261
  53.1 0.8 %copy.9 = bf16[4,512,128]{2,1,0:T(8,128)(2,1)} copy(bf16[4,512,128]{2,1,0:T(8,128)(2,1)S(1)} %shard_map.73) | data formatting | bytes 1048576
